TPU v7x, 256 devices: a whole 4x4x8 slice. The times are simulated.
256 devices in a mesh: seq: 32 (over x, z), head: 8 (over y, core).
Axes of the slice: x: 4, y: 4, z: 8, core: 2. Of those that a mesh axis runs over, the one named last changes fastest.
Arguments:
- inner_input: bfloat16 [16384, 16384], P('seq', 'head'), may hold values from -6 to 6
- state_input: bfloat16 [16384, 4096], P('seq', 'head'), may hold values from -6 to 6
- gate_input: bfloat16 [16384, 16384], P('seq', 'head'), may hold values from -6 to 6
- inner_taps: bfloat16 [4, 16384], P(None, 'head'), may hold values from -3 to 3
- inner_bias: bfloat16 [16384], P('head'), may hold values from -3 to 3
- state_taps: bfloat16 [4, 4096], P(None, 'head'), may hold values from -3 to 3
- state_bias: bfloat16 [4096], P('head'), may hold values from -3 to 3
- step_raw: float32 [256, 16384], P('head', 'seq'), may hold values from -5.3 to -1
- step_bias: float32 [256], P('head'), may hold values from -0.5 to 0.5
- decay_log: float32 [256], P('head'), may hold values from -9 to 1.26
- skip_gain: float32 [256], P('head'), may hold values from 0.5 to 1.5
- norm_gain: bfloat16 [16384], P('head'), may hold values from 0.5 to 1.5
- out_weight: bfloat16 [16384, 4096], P('head', 'seq'), may hold values from -0.09375 to 0.09375
- sequence_lengths: int32 [4], replicated, may hold values from 1 to 8192, 16384 in all
Outputs:
- mixed_out: bfloat16 [16384, 4096], P('seq', 'head')
Inputs may be any that keep to these rules, and one draw needn't show every extreme that they name: `sequence_lengths`: the 4 sequences lie end to end in the order given and fill all 16384 positions; the longest has exactly 8192 positions.
All inputs are finite; a program needn't handle non-finite values.
Results may differ from a plain program's by a relative error of at most 0.018.
Values may be sent and summed in bfloat16 or wider, within the bound.
No kernel may reach another device: no remote copies, remote signals or barrier semaphores. Data moves between devices by JAX's collectives and lax.ppermute only.
A program may use at most 256 MiB of HBM per device.

v0:
```python
import jax
import jax.numpy as jnp
import numpy as np
from jax import lax
from jax.sharding import Mesh
from jax.sharding import PartitionSpec as P

HEAD_DIM = 64
STATE_DIM = 256
BLOCK_LEN = 256
HIGHEST = lax.Precision.HIGHEST
EPSILON = 1e-05
SEQ = ("sx", "sz")


def segment_of(positions, sequence_lengths):
    starts = jnp.cumsum(sequence_lengths) - sequence_lengths
    hits = (positions[:, None] >= starts[None, :]).astype(jnp.int32)
    return jnp.sum(hits, axis=1) - 1


def causal_conv(extended, seg_extended, tap_table, bias_row):
    tap_count = tap_table.shape[0]
    length = extended.shape[0] - tap_count + 1
    current = seg_extended[tap_count - 1 :]
    summed = jnp.zeros((length, bias_row.shape[0]), jnp.float32) + bias_row.astype(jnp.float32)
    for start_shift in range(tap_count):
        kept_mask = (seg_extended[start_shift : start_shift + length] == current).astype(
            jnp.float32
        )
        summed = (
            summed
            + tap_table[start_shift].astype(jnp.float32)
            * extended[start_shift : start_shift + length].astype(jnp.float32)
            * kept_mask[:, None]
        )
    return jax.nn.silu(summed).astype(jnp.bfloat16)


def exclusive_weights(factors, place):
    n = factors.shape[0]
    idx = jnp.arange(n)
    j = idx[:, None]
    t = idx[None, :]
    between = (t > j) & (t < place)
    prods = jnp.prod(jnp.where(between[:, :, None], factors[None, :, :], 1.0), axis=1)
    return jnp.where((idx < place)[:, None], prods, 0.0)


def pack_state(state, factor):
    heads = factor.shape[0]
    flat = state.reshape(-1, state.shape[-1])
    extra = jnp.zeros((8, flat.shape[1]), jnp.float32).at[0, :heads].set(factor)
    return jnp.concatenate([flat, extra], axis=0).astype(jnp.bfloat16)


def unpack_state(gathered, heads):
    rows = gathered.shape[1] - 8
    states = (
        gathered[:, :rows]
        .astype(jnp.float32)
        .reshape(gathered.shape[0], heads, rows // heads, gathered.shape[2])
    )
    factors = gathered[:, rows, :heads].astype(jnp.float32)
    return (states, factors)


def combine(states, factors, place):
    weights = exclusive_weights(factors, place)
    return jnp.sum(weights[:, :, None, None] * states, axis=0)


def per_device(
    inner_input,
    state_input,
    gate_input,
    inner_taps,
    inner_bias,
    state_taps,
    state_bias,
    step_raw,
    step_bias,
    decay_log,
    skip_gain,
    norm_gain,
    out_weight,
    sequence_lengths,
):
    tok_rows = inner_input.shape[0]
    inner_width = inner_input.shape[1]
    heads = step_raw.shape[0]
    groups = state_input.shape[1] // (2 * STATE_DIM)
    per_group = heads // groups
    tap_count = inner_taps.shape[0]
    chunks = tok_rows // BLOCK_LEN
    L = BLOCK_LEN
    nz = lax.axis_size("sz")
    nseq = lax.axis_size("sx") * nz
    place = lax.axis_index("sx") * nz + lax.axis_index("sz")
    first_row = place * tok_rows
    weights = lax.all_gather(out_weight, SEQ, axis=1, tiled=True)
    positions = first_row + lax.iota(jnp.int32, tok_rows + tap_count - 1) - (tap_count - 1)
    seg_extended = segment_of(positions, sequence_lengths)
    seg_local = seg_extended[tap_count - 1 :]
    seg_before = seg_extended[tap_count - 2]
    tail_rows = jnp.concatenate(
        [inner_input[tok_rows - tap_count + 1 :], state_input[tok_rows - tap_count + 1 :]], axis=1
    )
    received = lax.ppermute(tail_rows, SEQ, [(s, s + 1) for s in range(nseq - 1)])
    inner_conv = causal_conv(
        jnp.concatenate([received[:, :inner_width], inner_input]),
        seg_extended,
        inner_taps,
        inner_bias,
    )
    state_conv = causal_conv(
        jnp.concatenate([received[:, inner_width:], state_input]),
        seg_extended,
        state_taps,
        state_bias,
    )
    u = inner_conv.reshape(chunks, L, groups, per_group, HEAD_DIM)
    vectors = state_conv.reshape(chunks, L, groups, 2, STATE_DIM)
    write_b = vectors[:, :, :, 0]
    read_c = vectors[:, :, :, 1]
    steps = jax.nn.softplus(step_raw + step_bias[:, None]).reshape(groups, per_group, chunks, L)
    rates = jnp.exp(decay_log).reshape(groups, per_group)
    gains = skip_gain.reshape(groups, per_group)
    running = jnp.cumsum(-rates[..., None, None] * steps, axis=3)
    seg_c = seg_local.reshape(chunks, L)
    seg_prev = jnp.concatenate([seg_before[None], seg_c[:-1, L - 1]])
    alive = (seg_c == seg_prev[:, None]).astype(jnp.float32)
    last = running[..., L - 1 :]
    u32 = u.astype(jnp.float32)
    scaled = u32 * jnp.transpose(steps, (2, 3, 0, 1))[..., None]
    closing = (seg_c == seg_c[:, L - 1 :]).astype(jnp.float32) * jnp.exp(last - running)
    weighted = scaled * jnp.transpose(closing, (2, 3, 0, 1))[..., None]
    chunk_states = jnp.einsum(
        "cjghp,cjgn->cghpn", weighted, write_b.astype(jnp.float32), precision=HIGHEST
    )
    kept = alive[:, L - 1] * jnp.exp(last[..., 0])
    kept = jnp.transpose(kept, (2, 0, 1))
    shard_state = chunk_states[0]
    shard_factor = kept[0]
    for c in range(1, chunks):
        shard_state = kept[c][..., None, None] * shard_state + chunk_states[c]
        shard_factor = shard_factor * kept[c]
    packed, weights = lax.optimization_barrier(
        (pack_state(shard_state, shard_factor.reshape(-1)), weights)
    )
    row = lax.all_gather(packed, "sz")
    row_states, row_factors = unpack_state(row, heads)
    zpos = lax.axis_index("sz")
    in_row = combine(row_states, row_factors, zpos)
    row_decay = jnp.prod(jnp.where((jnp.arange(nz) < zpos)[:, None], row_factors, 1.0), axis=0)
    row_total = combine(row_states, row_factors, nz)
    row_total_factor = jnp.prod(row_factors, axis=0)
    rows = lax.all_gather(pack_state(row_total, row_total_factor), "sx")
    rows_states, rows_factors = unpack_state(rows, heads)
    before_rows = combine(rows_states, rows_factors, lax.axis_index("sx"))
    state_in = (row_decay[:, None, None] * before_rows + in_row).reshape(
        groups, per_group, HEAD_DIM, STATE_DIM
    )
    read32 = read_c.astype(jnp.float32)
    scores = jnp.einsum("cign,cjgn->gcij", read_c, write_b, preferred_element_type=jnp.float32)
    row_index = lax.broadcasted_iota(jnp.int32, (L, L), 0)
    col_index = lax.broadcasted_iota(jnp.int32, (L, L), 1)
    linked = (row_index >= col_index)[None] & (seg_c[:, :, None] == seg_c[:, None, :])
    spread = running[..., :, None] - running[..., None, :]
    decays = jnp.where(linked, jnp.exp(jnp.where(linked, spread, 0.0)), 0.0)
    within = jnp.einsum("ghcij,cjghp->cighp", decays * scores[:, None], scaled, precision=HIGHEST)
    entering = [state_in]
    for c in range(1, chunks):
        entering.append(kept[c - 1][..., None, None] * entering[-1] + chunk_states[c - 1])
    entering = jnp.stack(entering)
    carried = jnp.einsum("cign,cghpn->cighp", read32, entering, precision=HIGHEST)
    enter_scale = jnp.transpose(alive[None, None] * jnp.exp(running), (2, 3, 0, 1))
    outputs = within + carried * enter_scale[..., None] + gains[..., None] * u32
    y_all = outputs.reshape(tok_rows, groups, per_group * HEAD_DIM)
    gated = y_all * jax.nn.silu(gate_input.astype(jnp.float32)).reshape(
        tok_rows, groups, per_group * HEAD_DIM
    )
    mean_sq = jnp.mean(gated * gated, axis=2, keepdims=True)
    gain_rows = norm_gain.astype(jnp.float32).reshape(groups, per_group * HEAD_DIM)
    normed = (
        (gated * lax.rsqrt(mean_sq + EPSILON) * gain_rows)
        .astype(jnp.bfloat16)
        .reshape(tok_rows, inner_width)
    )
    partial_out = jnp.dot(normed, weights, preferred_element_type=jnp.float32)
    return lax.psum_scatter(
        partial_out.astype(jnp.bfloat16), "head", scatter_dimension=1, tiled=True
    )


def split_seq(mesh):
    seq_devices = mesh.devices[:, 0]
    try:
        nx = len({d.coords[0] for d in seq_devices})
    except AttributeError:
        nx = 1
    nseq = seq_devices.shape[0]
    return Mesh(mesh.devices.reshape(nx, nseq // nx, mesh.devices.shape[1]), ("sx", "sz", "head"))


def solution(mesh):
    inner = split_seq(mesh)
    in_specs = (
        P(SEQ, "head"),
        P(SEQ, "head"),
        P(SEQ, "head"),
        P(None, "head"),
        P("head"),
        P(None, "head"),
        P("head"),
        P("head", SEQ),
        P("head"),
        P("head"),
        P("head"),
        P("head"),
        P("head", SEQ),
        P(),
    )
    out_specs = P(SEQ, "head")
    return jax.shard_map(
        per_device, mesh=inner, in_specs=in_specs, out_specs=out_specs, check_vma=False
    )
```

profile of v0, /device:TPU:2, one launch (start us, length us, event | category | flops | bytes accessed | tf_op | source)
XLA Modules:
  0.0 402.9 jit_solution(4032910775150019644)
XLA Ops:
  6.5 0.7 all-gather.5.cloned.1.call-update
  7.3 0.7 slice.163
  8.0 0.8 slice.162
  8.8 3.8 collective-permute-start
  12.6 0.8 reduce-window.19
  13.5 0.7 bitcast_subtract_fusion
  14.9 1.0 compare_select_fusion
  15.9 0.7 exponential_negate_fusion
  16.6 1.2 reduce-window.20
  18.5 1.3 pad_add_fusion
  21.4 0.8 slice_convert_fusion.8
  22.5 0.9 slice_convert_fusion.3
  24.0 2.9 copy.134
  26.9 0.7 reshape.721
  28.1 6.8 %fusion.31 = f32[512,2048]{0,1:T(8,128)} fusion(bf16[512,2048]{0,1:T(8,128)(2,1)S(1)} %copy.134, f32[2048]{0:T(1024)S(1)} %bitcast.130, f32[512]{0:T(512)S(1)} %get-tuple-element.54, bf16[3,2048]{0,1:T(8,128)(2,1)S(1)} %copy.133, f32[2048]{0:T(1024)S(1)} %bitcast.131, f32[512]{0:T(512)S(1)} %get-tuple-element.55, f32[2048]{0:T(1024)S(1)} %bitcast.129, ...), kind=kLoop, calls=%fused_computation.54 | loop fusion | flops 31457280 | bytes 6350848 | tf_op jit(solution)/shard_map/convert_element_type | solution.py:134
  34.9 5.9 %reshape.740 = f32[2,256,32,64]{1,0,3,2:T(2,128)} reshape(f32[512,2048]{0,1:T(8,128)} %fusion.31) | data formatting | bytes 8388608 | tf_op jit(solution)/shard_map/convert_element_type | solution.py:134
  40.9 0.9 multiply_convert_fusion.3
  41.9 0.7 fusion.55
  42.6 9.1 %broadcast_multiply_fusion = (f32[2,256,32,64]{1,0,3,2:T(2,128)S(1)}, f32[2,256,32,64]{1,0,3,2:T(2,128)}) fusion(f32[2,256,32]{1,0,2:T(2,128)S(1)} %copy.147, f32[2,256,32,64]{1,0,3,2:T(2,128)} %reshape.740, f32[2,256,32]{1,0,2:T(2,128)S(1)} %bitcast.126), kind=kLoop, calls=%fused_computation.52 | loop fusion | flops 2097152 | bytes 12713984 | tf_op jit(solution)/shard_map/mul | solution.py:137
  51.7 2.1 fusion.22
  53.8 1.9 copy-done
  55.9 1.1 fusion.32
  57.0 104.4 %all-gather.5.cloned.1.call-done = bf16[2048,4096]{1,0:T(8,128)(2,1)} async-done(((bf16[2048,128]{1,0:T(8,128)(2,1)}), bf16[2048,4096]{1,0:T(8,128)(2,1)}) %all-gather.5.cloned.1.call-update) | async-done | bytes 16777232 | tf_op jit(solution)/shard_map/all_gather | solution.py:101
  161.8 93.9 %all-gather.9.cloned.1.call-done = bf16[16448,256]{1,0:T(8,128)(2,1)} async-done(((bf16[2056,256]{1,0:T(8,128)(2,1)}), bf16[16448,256]{1,0:T(8,128)(2,1)}) %all-gather.9.cloned.1.call-update) | async-done | bytes 8421392 | tf_op jit(solution)/shard_map/all_gather | solution.py:151
  255.7 0.7 slice_reduce_fusion.2
  256.6 0.7 select_reduce_fusion.3
  257.5 0.7 mul.529
  258.3 11.2 %fusion = (bf16[2048,256]{1,0:T(8,128)(2,1)S(1)}, f32[2048,256]{1,0:T(8,128)S(1)}) fusion(f32[8,2048]{1,0:T(8,128)S(1)} %mul.520, bf16[8,2056,256]{2,1,0:T(8,128)(2,1)} %bitcast.122, f32[8,2048]{1,0:T(8,128)} %mul.529), kind=kLoop, calls=%fused_computation.2 | loop fusion | flops 19922944 | bytes 11665408 | tf_op jit(solution)/shard_map/reduce_sum | solution.py:70
  269.4 1.1 pad_maximum_fusion.1
  270.6 0.7 convert_element_type.187
  271.3 0.7 reshape.723
  272.0 0.8 broadcast.372
  272.8 1.0 copy.157
  274.0 4.0 copy.154
  278.2 6.1 %reshape.746 = f32[2,256,1,32,64]{1,0,4,3,2:T(2,128)} reshape(f32[512,2048]{0,1:T(8,128)} %fusion.31) | data formatting | bytes 8388608 | tf_op jit(solution)/shard_map/convert_element_type | solution.py:134
  284.5 21.5 %fusion.2 = f32[2,32,64,256]{3,2,1,0:T(8,128)} fusion(f32[2,256,256]{2,1,0:T(8,128)S(1)} %fusion.37, f32[32,2,256]{2,0,1:T(8,128)S(1)} %reduce_window_sum.47, pred[2,256,256]{2,1,0:T(8,128)(4,1)S(1)} %compare_and_fusion, f32[2,256,32,64]{1,0,3,2:T(2,128)} %get-tuple-element.40), kind=kOutput, calls=%fused_computation.4 | convolution fusion | flops 3238002688 | bytes 9109504 | tf_op jit(solution)/shard_map/ghcij,cjghp->cighp/dot_general | solution.py:171
  306.0 13.5 %all-gather.7.cloned.1.call-done = bf16[4,2056,256]{2,1,0:T(8,128)(2,1)} async-done(((bf16[1,2056,256]{2,1,0:T(8,128)(2,1)}), bf16[4,2056,256]{2,1,0:T(8,128)(2,1)}) %all-gather.7.cloned.1.call-update) | async-done | bytes 4210704 | tf_op jit(solution)/shard_map/all_gather | solution.py:158
  319.5 0.7 slice_convert_fusion.4
  320.6 3.2 multiply_reduce_fusion
  324.1 1.9 copy-done.1
  326.4 1.8 copy-done.2
  328.2 1.3 copy-done.4
  329.4 3.0 fusion.21
  332.5 3.3 copy.153
  336.3 1.1 copy-done.3
  337.4 1.4 multiply_reduce_fusion.1
  338.9 15.8 %convolution_convert_fusion = bf16[512,4096]{1,0:T(8,128)(2,1)} fusion(bf16[2048,4096]{1,0:T(8,128)(2,1)} %all-gather.5.cloned.1.call-done, f32[2048]{0:T(1024)S(1)} %convert_element_type.187, f32[512]{0:T(512)S(1)} %add_rsqrt_fusion, f32[512,2048]{0,1:T(8,128)S(1)} %bitcast.119, bf16[512,2048]{0,1:T(8,128)(2,1)S(1)} %copy-done.3), kind=kOutput, calls=%fused_computation.16 | convolution fusion | flops 8601468928 | bytes 27273216 | tf_op jit(solution)/shard_map/dot_general | solution.py:190
  354.6 41.7 %reduce-scatter.2.cloned.1.call-done = bf16[512,512]{1,0:T(8,128)(2,1)} async-done(((bf16[512,4096]{1,0:T(8,128)(2,1)}), bf16[512,512]{1,0:T(8,128)(2,1)}) %reduce-scatter.2.cloned.1.call-update) | async-done | bytes 524304 | tf_op jit(solution)/shard_map/reduce_scatter | solution.py:191
  (91 shorter events, 7.7 us)
Async XLA Ops:
  6.5 21.1 %copy-start.9 = (bf16[2048]{0:T(1024)(128)(2,1)S(1)}, bf16[2048]{0:T(1024)(128)(2,1)}, u32[]{:S(2)}) copy-start(bf16[2048]{0:T(1024)(128)(2,1)} %param.22) | copy-start | bytes 12292
  6.5 21.2 %copy-start.12 = (bf16[512]{0:T(512)(128)(2,1)S(1)}, bf16[512]{0:T(512)(128)(2,1)}, u32[]{:S(2)}) copy-start(bf16[512]{0:T(512)(128)(2,1)} %param.24) | copy-start | bytes 3076
  6.5 154.9 %all-gather.5.cloned.1.call-start = ((), (), s32[]{:S(2)}) async-start(), calls=%async_computation.1 | async-start | bytes 17301504 | tf_op jit(solution)/shard_map/all_gather | solution.py:101
  7.3 248.5 %all-gather.9.cloned.1.call-start = ((), (), s32[]{:S(2)}) async-start(), calls=%async_computation.4 | async-start | bytes 9474048 | tf_op jit(solution)/shard_map/all_gather | solution.py:151
  8.8 18.9 %collective-permute-start = (bf16[3,2560]{1,0:T(4,128)(2,1)S(1)}, bf16[3,2560]{1,0:T(4,128)(2,1)S(1)}, u32[]{:S(2)}, u32[]{:S(2)}) collective-permute-start(bf16[3,2560]{1,0:T(4,128)(2,1)S(1)} %pad_maximum_fusion.3), channel_id=1, source_target_pairs={{0,8},{8,16},{16,24},{24,32},{32,40},{40,48},{48,56},{56,64},{64,7... | collective-permute-start | bytes 46088 | tf_op jit(solution)/shard_map/ppermute | solution.py:109
  34.9 6.0 %copy-start.5 = (bf16[512,512]{1,0:T(8,128)(2,1)S(1)}, bf16[512,512]{1,0:T(8,128)(2,1)}, u32[]{:S(2)}) copy-start(bf16[512,512]{1,0:T(8,128)(2,1)} %param.19) | copy-start | bytes 1572868
  40.8 1.8 copy-start.6
  53.7 1.9 copy-start
  161.5 158.0 %all-gather.7.cloned.1.call-start = ((), (), s32[]{:S(2)}) async-start(), calls=%async_computation.2 | async-start | bytes 5263360 | tf_op jit(solution)/shard_map/all_gather | solution.py:158
  270.5 125.8 %reduce-scatter.2.cloned.1.call-start = ((), (), s32[]{:S(2)}) async-start(), calls=%async_computation.3 | async-start | bytes 4718592 | tf_op jit(solution)/shard_map/reduce_scatter | solution.py:191
  273.9 4.0 copy-start.7
  306.0 17.8 %copy-start.8 = (f32[32]{0:T(128)S(1)}, f32[32]{0:T(128)}, u32[]{:S(2)}) copy-start(f32[32]{0:T(128)} %get-tuple-element.61) | copy-start | bytes 388
  323.8 2.2 copy-start.1
  323.8 2.2 copy-start.11
  326.0 2.2 copy-start.2
  326.0 3.5 copy-start.4
  326.0 3.5 copy-start.10
  335.8 1.6 copy-start.3
Sparse Core Ops, SparseCore 0:
  9.8 151.6 all-gather.4
  163.3 92.4 all-gather.8
  270.6 48.8 all-gather.6
  354.8 41.5 reduce-scatter.1
where the time goes:
time: 404 us; the launch traced here: 403 us
  waiting for transfers between devices  254 us (63%)
  other arithmetic  47.9 us (12%)
  matrix products  42.6 us (11%)
  local copies, waits for them, and re-layouts  40.3 us (10%)
  between operations  13.6 us (3%)
  starting transfers between devices  4.13 us (1%)
    all_gather x1, waiting for transfers between devices, per_device(): weights = lax.all_gather(out_weight, SEQ, axis=1, tiled=True)  104 us
    all_gather x1, waiting for transfers between devices, per_device(): row = lax.all_gather(packed, 'sz')  93.9 us
    reduce_scatter x1, waiting for transfers between devices, per_device(): lax.psum_scatter(partial_out.astype(jnp.bfloat16), 'head', scatter_dimens...  41.7 us
    dot_general x1, matrix products, per_device(): jnp.einsum('ghcij,cjghp->cighp', decays * scores[:, None], scaled, precis...  21.5 us
    dot_general x1, matrix products, per_device(): partial_out = jnp.dot(normed, weights, preferred_element_type=jnp.float32)  15.8 us
    unnamed x29, local copies, waits for them, and re-layouts  15.3 us
    reduce_sum x2, other arithmetic, combine(): return jnp.sum(weights[:, :, None, None] * states, axis=0)  14.4 us
    all_gather x1, waiting for transfers between devices, per_device(): rows = lax.all_gather(pack_state(row_total, row_total_factor), 'sx')  13.5 us
  transfers between devices with their start and end apart: 5, of which 4 were waited for; matrix products, arithmetic and copies ran while one was open for 20% of the time, Pallas kernels for 0%

commit v1 on v0

--- a/solution.py
+++ b/solution.py
@@ -98,7 +98,9 @@
     nseq = lax.axis_size("sx") * nz
     place = lax.axis_index("sx") * nz + lax.axis_index("sz")
     first_row = place * tok_rows
-    weights = lax.all_gather(out_weight, SEQ, axis=1, tiled=True)
+    weights = jnp.concatenate(
+        lax.all_to_all(jnp.stack([out_weight] * lax.axis_size(SEQ)), SEQ, 0, 0), axis=1
+    )
     positions = first_row + lax.iota(jnp.int32, tok_rows + tap_count - 1) - (tap_count - 1)
     seg_extended = segment_of(positions, sequence_lengths)
     seg_local = seg_extended[tap_count - 1 :]

time: 404 us -> 709 us (1.75)
  waiting for transfers between devices: 254 us -> 539 us
  starting transfers between devices: 4.13 us -> 15.5 us
  local copies, waits for them, and re-layouts: 40.3 us -> 49 us
    ppermute x1, waiting for transfers between devices: 0.01 us -> 391 us  [per_device(): lax.ppermute(tail_rows, SEQ, [(s, s + 1) for s in range(nseq - 1)])]
    all_gather x1 -> x0, waiting for transfers between devices: 104 us -> none  [per_device(): weights = lax.all_gather(out_weight, SEQ, axis=1, tiled=True)]
    all_to_all x0 -> x1, starting transfers between devices: none -> 11.8 us  [per_device(): lax.all_to_all(jnp.stack([out_weight] * lax.axis_size(SEQ)), SEQ, 0, 0)]
    another operation x10 -> x11, local copies, waits for them, and re-layouts: 2.94 us -> 10.4 us  [the longest x1 5.96 us: per_device(): jnp.stack([out_weight] * lax.axis_size(SEQ))]
    unnamed x29 -> x70, local copies, waits for them, and re-layouts: 15.3 us -> 17.2 us
  transfers between devices with their start and end apart: 5 -> 5, of which waited for: 4 -> 4; matrix products, arithmetic and copies ran while one was open for 20% -> 11% of each run, Pallas kernels for 0% -> 0%
where the time goes in v1:
time: 709 us; the launch traced here: 708 us
  waiting for transfers between devices  539 us (76%)
  local copies, waits for them, and re-layouts  49 us (7%)
  other arithmetic  46.5 us (7%)
  matrix products  43.7 us (6%)
  starting transfers between devices  15.5 us (2%)
  between operations  13.8 us (2%)
    ppermute x1, waiting for transfers between devices, per_device(): lax.ppermute(tail_rows, SEQ, [(s, s + 1) for s in range(nseq - 1)])  391 us
    all_gather x1, waiting for transfers between devices, per_device(): row = lax.all_gather(packed, 'sz')  94.1 us
    reduce_scatter x1, waiting for transfers between devices, per_device(): lax.psum_scatter(partial_out.astype(jnp.bfloat16), 'head', scatter_dimens...  41.7 us
    dot_general x1, matrix products, per_device(): jnp.einsum('ghcij,cjghp->cighp', decays * scores[:, None], scaled, precis...  21.5 us
    unnamed x70, local copies, waits for them, and re-layouts  17.2 us
    dot_general x1, matrix products, per_device(): partial_out = jnp.dot(normed, weights, preferred_element_type=jnp.float32)  16.8 us
    reduce_sum x2, other arithmetic, combine(): return jnp.sum(weights[:, :, None, None] * states, axis=0)  14.4 us
  transfers between devices with their start and end apart: 5, of which 4 were waited for; matrix products, arithmetic and copies ran while one was open for 11% of the time, Pallas kernels for 0%

profile of v1, /device:TPU:2, one launch (start us, length us, event | category | flops | bytes accessed | tf_op | source)
XLA Modules:
  0.0 707.6 jit_solution(1846150978261678530)
XLA Ops:
  6.5 1.2 copy.154
  7.8 6.0 stack.6
  13.8 11.8 %all-to-all-start = ((bf16[32,2048,128]{1,2,0:T(8,128)(2,1)}), bf16[32,2048,128]{1,2,0:T(8,128)(2,1)}, u32[]{:S(2)}, u32[]{:S(2)}) async-start(bf16[32,2048,128]{1,2,0:T(8,128)(2,1)} %stack.6), calls=%async_computation | async-start | bytes 33554432 | tf_op jit(solution)/shard_map/all_to_all | solution.py:102
  25.7 0.8 slice.162
  26.5 3.4 collective-permute-start
  31.1 1.1 reduce-window.20
  33.0 1.3 pad_add_fusion
  35.8 0.7 fusion.47
  36.5 0.6 slice_convert_fusion.8
  37.4 0.6 slice_convert_fusion.3
  38.6 2.9 copy.139
  41.5 0.7 reshape.729
  42.3 0.6 convert_element_type.158
  43.5 391.4 %collective-permute-done = bf16[3,2560]{1,0:T(4,128)(2,1)S(1)} collective-permute-done((bf16[3,2560]{1,0:T(4,128)(2,1)S(1)}, bf16[3,2560]{1,0:T(4,128)(2,1)S(1)}, u32[]{:S(2)}, u32[]{:S(2)}) %collective-permute-start) | collective-permute-done | bytes 15392 | tf_op jit(solution)/shard_map/ppermute | solution.py:111
  434.9 0.6 copy-done.12
  435.8 7.5 %fusion.31 = f32[512,2048]{0,1:T(8,128)} fusion(bf16[512,2048]{0,1:T(8,128)(2,1)S(1)} %copy.139, f32[2048]{0:T(1024)} %bitcast.133, f32[512]{0:T(512)} %get-tuple-element.54, bf16[3,2048]{0,1:T(8,128)(2,1)S(1)} %copy.138, f32[2048]{0:T(1024)} %bitcast.134, f32[512]{0:T(512)} %get-tuple-element.55, f32[2048]{0:T(1024)} %bitcast.132, ...), kind=kLoop, calls=%fused_computation.54 | loop fusion | flops 31457280 | bytes 6350848 | tf_op jit(solution)/shard_map/convert_element_type | solution.py:136
  443.4 5.9 reshape.750
  449.4 0.9 multiply_convert_fusion.3
  450.4 0.7 fusion.55
  451.1 9.0 %broadcast_multiply_fusion = (f32[2,256,32,64]{1,0,3,2:T(2,128)S(1)}, f32[2,256,32,64]{1,0,3,2:T(2,128)}) fusion(f32[2,256,32]{1,0,2:T(2,128)S(1)} %copy.152, f32[2,256,32,64]{1,0,3,2:T(2,128)} %reshape.750, f32[2,256,32]{1,0,2:T(2,128)S(1)} %bitcast.129), kind=kLoop, calls=%fused_computation.52 | loop fusion | flops 2097152 | bytes 12713984 | tf_op jit(solution)/shard_map/mul | solution.py:139
  460.1 2.1 fusion.22
  462.2 1.9 copy-done
  464.4 1.1 fusion.32
  465.8 94.1 %all-gather.6.cloned.1.call-done = bf16[16448,256]{1,0:T(8,128)(2,1)} async-done(((bf16[2056,256]{1,0:T(8,128)(2,1)}), bf16[16448,256]{1,0:T(8,128)(2,1)}) %all-gather.6.cloned.1.call-update) | async-done | bytes 8421392 | tf_op jit(solution)/shard_map/all_gather | solution.py:153
  559.9 0.7 slice_reduce_fusion.2
  561.1 0.7 mul.529
  561.8 11.2 %fusion = (bf16[2048,256]{1,0:T(8,128)(2,1)S(1)}, f32[2048,256]{1,0:T(8,128)S(1)}) fusion(f32[8,2048]{1,0:T(8,128)S(1)} %mul.520, bf16[8,2056,256]{2,1,0:T(8,128)(2,1)} %bitcast.125, f32[8,2048]{1,0:T(8,128)} %mul.529), kind=kLoop, calls=%fused_computation.2 | loop fusion | flops 19922944 | bytes 11665408 | tf_op jit(solution)/shard_map/reduce_sum | solution.py:70
  573.0 1.1 pad_maximum_fusion.1
  574.2 0.7 copy.142
  574.8 0.8 broadcast.374
  575.6 1.0 copy.163
  576.7 1.5 reshape.731
  578.3 4.0 copy.160
  582.3 0.7 convert_element_type.187
  583.2 6.1 reshape.756
  589.6 21.5 %fusion.2 = f32[2,32,64,256]{3,2,1,0:T(8,128)} fusion(f32[2,256,256]{2,1,0:T(8,128)S(1)} %fusion.37, f32[32,2,256]{2,0,1:T(8,128)S(1)} %reduce_window_sum.47, pred[2,256,256]{2,1,0:T(8,128)(4,1)S(1)} %compare_and_fusion, f32[2,256,32,64]{1,0,3,2:T(2,128)} %get-tuple-element.40), kind=kOutput, calls=%fused_computation.4 | convolution fusion | flops 3238002688 | bytes 9109504 | tf_op jit(solution)/shard_map/ghcij,cjghp->cighp/dot_general | solution.py:173
  611.1 12.0 %all-gather.4.cloned.1.call-done = bf16[4,2056,256]{2,1,0:T(8,128)(2,1)} async-done(((bf16[1,2056,256]{2,1,0:T(8,128)(2,1)}), bf16[4,2056,256]{2,1,0:T(8,128)(2,1)}) %all-gather.4.cloned.1.call-update) | async-done | bytes 4210704 | tf_op jit(solution)/shard_map/all_gather | solution.py:160
  623.1 0.7 slice_convert_fusion.4
  624.1 3.2 multiply_reduce_fusion
  627.7 1.9 copy-done.1
  630.0 1.8 copy-done.2
  631.7 1.3 copy-done.4
  633.0 3.0 fusion.21
  636.1 3.4 copy.159
  639.9 1.1 copy-done.3
  641.1 1.4 multiply_reduce_fusion.1
  642.5 16.8 %convolution_convert_fusion = bf16[512,4096]{1,0:T(8,128)(2,1)} fusion(bf16[2048,4096]{0,1:T(8,128)(2,1)} %bitcast.33, f32[2048]{0:T(1024)S(1)} %convert_element_type.187, f32[512]{0:T(512)S(1)} %add_rsqrt_fusion, f32[512,2048]{0,1:T(8,128)S(1)} %bitcast.122, bf16[512,2048]{0,1:T(8,128)(2,1)} %copy.160), kind=kOutput, calls=%fused_computation.16 | convolution fusion | flops 8601468928 | bytes 27273216 | tf_op jit(solution)/shard_map/dot_general | solution.py:192
  659.3 41.7 %reduce-scatter.2.cloned.1.call-done = bf16[512,512]{1,0:T(8,128)(2,1)} async-done(((bf16[512,4096]{1,0:T(8,128)(2,1)}), bf16[512,512]{1,0:T(8,128)(2,1)}) %reduce-scatter.2.cloned.1.call-update) | async-done | bytes 524304 | tf_op jit(solution)/shard_map/reduce_scatter | solution.py:193
  (133 shorter events, 8.7 us)
Async XLA Ops:
  13.7 12.7 %copy-start.5 = (bf16[512,512]{1,0:T(8,128)(2,1)S(1)}, bf16[512,512]{1,0:T(8,128)(2,1)}, u32[]{:S(2)}) copy-start(bf16[512,512]{1,0:T(8,128)(2,1)} %param.19) | copy-start | bytes 1572868
  13.8 16.2 %copy-start.31 = (s32[4]{0:T(128)S(1)}, s32[4]{0:T(128)}, u32[]{:S(2)}) copy-start(s32[4]{0:T(128)} %param.31) | copy-start | bytes 52
  13.8 17.1 %copy-start.8 = (f32[32,512]{1,0:T(8,128)S(1)}, f32[32,512]{1,0:T(8,128)}, u32[]{:S(2)}) copy-start(f32[32,512]{1,0:T(8,128)} %param.25) | copy-start | bytes 196612
  13.8 17.1 %copy-start.30 = (f32[32]{0:T(128)S(1)}, f32[32]{0:T(128)}, u32[]{:S(2)}) copy-start(f32[32]{0:T(128)} %param.26) | copy-start | bytes 388
  13.8 17.3 %copy-start.32 = (f32[32]{0:T(128)S(1)}, f32[32]{0:T(128)}, u32[]{:S(2)}) copy-start(f32[32]{0:T(128)} %param.27) | copy-start | bytes 388
  13.8 22.7 %copy-start.18 = (bf16[4,512]{1,0:T(4,128)(2,1)S(1)}, bf16[4,512]{1,0:T(4,128)(2,1)}, u32[]{:S(2)}) copy-start(bf16[4,512]{1,0:T(4,128)(2,1)} %param.23) | copy-start | bytes 12292
  13.8 23.6 %copy-start.9 = (bf16[4,2048]{1,0:T(4,128)(2,1)S(1)}, bf16[4,2048]{1,0:T(4,128)(2,1)}, u32[]{:S(2)}) copy-start(bf16[4,2048]{1,0:T(4,128)(2,1)} %param.21) | copy-start | bytes 49156
  13.8 451.7 %all-to-all-start = ((bf16[32,2048,128]{1,2,0:T(8,128)(2,1)}), bf16[32,2048,128]{1,2,0:T(8,128)(2,1)}, u32[]{:S(2)}, u32[]{:S(2)}) async-start(bf16[32,2048,128]{1,2,0:T(8,128)(2,1)} %stack.6), calls=%async_computation | async-start | bytes 33554432 | tf_op jit(solution)/shard_map/all_to_all | solution.py:102
  25.6 16.7 %copy-start.24 = (bf16[2048]{0:T(1024)(128)(2,1)S(1)}, bf16[2048]{0:T(1024)(128)(2,1)}, u32[]{:S(2)}) copy-start(bf16[2048]{0:T(1024)(128)(2,1)} %param.22) | copy-start | bytes 12292
  25.6 17.3 %copy-start.29 = (bf16[512]{0:T(512)(128)(2,1)S(1)}, bf16[512]{0:T(512)(128)(2,1)}, u32[]{:S(2)}) copy-start(bf16[512]{0:T(512)(128)(2,1)} %param.24) | copy-start | bytes 3076
  25.6 534.2 %all-gather.6.cloned.1.call-start = ((), (), s32[]{:S(2)}) async-start(), calls=%async_computation.4 | async-start | bytes 9474048 | tf_op jit(solution)/shard_map/all_gather | solution.py:153
  26.5 408.4 %collective-permute-start = (bf16[3,2560]{1,0:T(4,128)(2,1)S(1)}, bf16[3,2560]{1,0:T(4,128)(2,1)S(1)}, u32[]{:S(2)}, u32[]{:S(2)}) collective-permute-start(bf16[3,2560]{1,0:T(4,128)(2,1)S(1)} %pad_maximum_fusion.3), channel_id=1, source_target_pairs={{0,8},{8,16},{16,24},{24,32},{32,40},{40,48},{48,56},{56,64},{64,7... | collective-permute-start | bytes 46088 | tf_op jit(solution)/shard_map/ppermute | solution.py:111
  32.4 402.4 %copy-start.10 = (s32[2,256]{1,0:T(2,128)}, s32[2,256]{1,0:T(2,128)S(1)}, u32[]{:S(2)}) copy-start(s32[2,256]{1,0:T(2,128)S(1)} %eq.58) | copy-start | bytes 6148
  34.9 3.2 copy-start.16
  434.9 0.6 copy-start.12
  443.4 5.9 slice-start
  443.4 5.9 copy-start.13
  443.4 5.9 copy-start.14
  443.4 5.9 copy-start.15
  443.4 5.9 copy-start.19
  443.4 5.9 copy-start.20
  443.4 5.9 copy-start.21
  443.4 5.9 copy-start.22
  443.4 5.9 copy-start.23
  449.3 1.8 copy-start.6
  460.1 4.0 copy-start.28
  462.2 2.0 copy-start
  462.2 2.2 copy-start.27
  465.5 157.6 %all-gather.4.cloned.1.call-start = ((), (), s32[]{:S(2)}) async-start(), calls=%async_computation.2 | async-start | bytes 5263360 | tf_op jit(solution)/shard_map/all_gather | solution.py:160
  561.8 13.0 %copy-start.17 = (f32[32,2,2]{0,1,2:T(2,128)S(1)}, f32[32,2,2]{0,1,2:T(2,128)}, u32[]{:S(2)}) copy-start(f32[32,2,2]{0,1,2:T(2,128)} %copy-done.16) | copy-start | bytes 1540
  573.0 10.0 %copy-start.11 = (s32[2,256]{1,0:T(2,128)S(1)}, s32[2,256]{1,0:T(2,128)}, u32[]{:S(2)}) copy-start(s32[2,256]{1,0:T(2,128)} %copy-done.10) | copy-start | bytes 6148
  574.1 126.9 %reduce-scatter.2.cloned.1.call-start = ((), (), s32[]{:S(2)}) async-start(), calls=%async_computation.3 | async-start | bytes 4718592 | tf_op jit(solution)/shard_map/reduce_scatter | solution.py:193
  578.3 4.7 copy-start.7
  627.4 2.2 copy-start.1
  627.4 2.2 copy-start.26
  629.6 2.2 copy-start.2
  629.6 3.5 copy-start.4
  629.6 3.5 copy-start.25
  639.5 1.6 copy-start.3
Sparse Core Ops, SparseCore 0:
  465.6 94.1 all-gather.5
  574.2 48.8 all-gather.3
  659.5 41.5 reduce-scatter.1
